TPU v7x, 32 devices: a whole 2x2x4 slice. The times are simulated.
32 devices in a mesh: high: 8 (over z, core), low: 4 (over y, x).
Axes of the slice: x: 2, y: 2, z: 4, core: 2. Of those that a mesh axis runs over, the one named last changes fastest.
Arguments:
- wave_parts: float32 [2, 128, 128, 128], P(None, ('high', 'low')), may hold values from -6 to 6
- level_table: float32 [128, 128, 128], P(('high', 'low')), may hold values from -2 to 2
- phase_angles: float32 [2, 128], replicated, may hold values from 0.3 to 1.2
- mix_angles: float32 [2, 4], replicated, may hold values from 0.3 to 1.2
Outputs:
- result_parts: float32 [2, 128, 128, 128], P(None, ('high', 'low'))
- marginal: float32 [16, 128, 128], P('low', 'high')
All inputs are finite; a program needn't handle non-finite values.
Results may differ from a plain program's by a relative error of at most 0.0003.
Values sent between devices are 32-bit elements; how exact they have to be, the bound alone decides.
A program may use at most 64 MiB of HBM per device.

v0:
```python
import functools

import jax
import jax.numpy as jnp
from jax import lax
from jax.experimental import pallas as pl
from jax.experimental.pallas import tpu as pltpu
from jax.sharding import PartitionSpec as P

LAYERS = 2
MESH = pl.DeviceIdType.MESH
SUBLANES = 8


def count_bits(values, count):
    places = jnp.arange(count.bit_length() - 1, dtype=jnp.int32)
    return jnp.sum(values[..., None] >> places & 1, axis=-1)


def real_turn_table(count, angle):
    rank = jnp.arange(count, dtype=jnp.int32)
    apart = count_bits(rank[:, None] ^ rank[None, :], count)
    minus = count_bits(rank[:, None] & (rank[:, None] ^ rank[None, :]), count)
    bits = count.bit_length() - 1
    size = jnp.cos(angle) ** (bits - apart).astype(jnp.float32) * jnp.sin(angle) ** apart.astype(
        jnp.float32
    )
    return size * jnp.where(minus % 2 == 1, -1.0, 1.0).astype(jnp.float32)


def apply_along(values, dim, angle):
    real_part = real_turn_table(values.shape[dim], angle)
    moved = jnp.tensordot(values, real_part, axes=([dim], [0]), precision=lax.Precision.HIGHEST)
    return jnp.moveaxis(moved, -1, dim)


def phase_step(values, levels, angle):
    turn = angle * levels
    return jnp.stack(
        [
            values[0] * jnp.cos(turn) + values[1] * jnp.sin(turn),
            values[1] * jnp.cos(turn) - values[0] * jnp.sin(turn),
        ]
    )


def by_axis(wave_parts, level_table, phase_angles, mix_angles):
    values = wave_parts
    for layer in range(LAYERS):
        values = phase_step(values, level_table, phase_angles[layer])
        values = apply_along(values, 3, mix_angles[layer, 0])
        values = apply_along(values, 2, mix_angles[layer, 1])
        values = apply_along(values, 1, mix_angles[layer, 2])
        moved = lax.all_to_all(values, "high", split_axis=2, concat_axis=1, tiled=True)
        spread = moved.reshape(2, lax.axis_size("high"), -1, moved.shape[2], moved.shape[3])
        moved = apply_along(spread, 1, mix_angles[layer, 2]).reshape(moved.shape)
        values = lax.all_to_all(moved, "high", split_axis=1, concat_axis=2, tiled=True)
        moved = lax.all_to_all(values, "low", split_axis=3, concat_axis=1, tiled=True)
        spread = moved.reshape(2, lax.axis_size("low"), -1, moved.shape[2], moved.shape[3])
        moved = apply_along(spread, 1, mix_angles[layer, 3]).reshape(moved.shape)
        values = lax.all_to_all(moved, "low", split_axis=1, concat_axis=3, tiled=True)
    chance = values[0] * values[0] + values[1] * values[1]
    marginal = lax.psum_scatter(chance, "high", scatter_dimension=1, tiled=True) / lax.axis_size(
        "high"
    )
    return (values, marginal)


def mix_list(values, groups):
    values = list(values)
    stride = 1
    for bits, cos, sin in groups:
        for _ in range(bits):
            for at in range(len(values)):
                if at & stride == 0:
                    u, v = values[at], values[at + stride]
                    values[at] = cos * u - sin * v
                    values[at + stride] = cos * v + sin * u
            stride *= 2
    return values


def turn_matrix(groups, sign):
    size = 1
    for bits, _, _ in groups:
        size <<= bits
    row = lax.broadcasted_iota(jnp.int32, (size, size), 0)
    column = lax.broadcasted_iota(jnp.int32, (size, size), 1)
    out = None
    place = 0
    for bits, cos, sin in groups:
        up = sign * sin
        for _ in range(bits):
            kb = (row >> place) & 1
            nb = (column >> place) & 1
            factor = jnp.where(kb == nb, cos, jnp.where(nb > kb, up, -up))
            out = factor if out is None else out * factor
            place += 1
    return out


def split(values):
    high = values.astype(jnp.bfloat16)
    return high, (values - high.astype(jnp.float32)).astype(jnp.bfloat16)


def product(left, right):
    dot = functools.partial(jnp.dot, preferred_element_type=jnp.float32)
    return dot(left[0], right[0]) + (dot(left[1], right[0]) + dot(left[0], right[1]))


def log2(count):
    return count.bit_length() - 1


def turn_chunks(ref, t, h, part, pair):
    chunks = part // SUBLANES
    at = [pl.ds(h * part + j * SUBLANES, SUBLANES) for j in range(chunks)]
    return [mix_list([ref[p, t, r, :] for r in at], [(log2(chunks), *pair)]) for p in range(2)]


def finish(n_high, mix_ref, back, gathered, out_ref, marginal_ref):
    _, blocks, rows, lanes = back.shape
    part = rows // n_high
    angle = jnp.full((SUBLANES, lanes), mix_ref[LAYERS - 1, 1], jnp.float32)
    pair = jnp.cos(angle), jnp.sin(angle)
    for t in range(blocks):
        for h in range(n_high):
            for p, values in enumerate(turn_chunks(back, t, h, part, pair)):
                for j, value in enumerate(values):
                    out_ref[p, t, pl.ds(h * part + j * SUBLANES, SUBLANES), :] = value
    total = gathered[0]
    for z in range(1, gathered.shape[0]):
        total = total + gathered[z]
    marginal_ref[...] = total * (1.0 / n_high)


def kernel(
    n_high, n_low,
    mix_ref, wave_hbm, level_hbm, phase_ref,
    back, gathered,
    wave_ref, level_ref, a_ref, b_ref, c_ref, level_b, chance, pair, sums,
    load_sem, send_sem, recv_state, recv_level, recv_back, recv_pair, recv_sums,
):
    loads = [
        pltpu.make_async_copy(level_hbm, level_ref, load_sem.at[0]),
        pltpu.make_async_copy(wave_hbm, wave_ref, load_sem.at[1]),
    ]
    for load in loads:
        load.start()
    _, blocks, rows, lanes = wave_ref.shape
    part = rows // n_high
    chunks = part // SUBLANES
    count = n_high * n_low
    twos = n_high // 2
    mh, ml = lax.axis_index("high"), lax.axis_index("low")

    barrier = pltpu.get_barrier_semaphore()

    def other(i):
        k = 1 + i
        return k, (mh + k // n_low) % n_high, (ml + k % n_low) % n_low

    @pl.loop(0, count - 1)
    def _(i):
        _, dh, dl = other(i)
        pl.semaphore_signal(barrier, inc=1, device_id=(dh, dl), device_id_type=MESH)

    def angles(layer, group):
        angle = jnp.full((SUBLANES, lanes), mix_ref[layer, group], jnp.float32)
        return jnp.cos(angle), jnp.sin(angle)

    def wide(pair, size):
        return tuple(jnp.broadcast_to(x[:1, :1], (size, size)) for x in pair)

    def phase(re, im, levels, layer):
        turn = phase_ref[pl.ds(layer, 1), :] * levels
        cos, sin = jnp.cos(turn), jnp.sin(turn)
        return re * cos + im * sin, im * cos - re * sin

    def tile(h, j):
        return pl.ds(pl.multiple_of(h * part + j * SUBLANES, SUBLANES), SUBLANES)

    def mix_in_a(ref, j, layer):
        row_pair, block_pair = angles(layer, 1), angles(layer, 2)
        groups = [(log2(n_high), *row_pair), (log2(blocks), *block_pair)]
        at = [(t, tile(h, j)) for t in range(blocks) for h in range(n_high)]
        for p in range(2):
            values = mix_list([ref[p, t, r, :] for t, r in at], groups)
            for (t, r), value in zip(at, values):
                ref[p, t, r, :] = value

    def mix_chunks(ref, t, h, layer):
        return turn_chunks(ref, t, h, part, angles(layer, 1))

    def tables(layer):
        lane = turn_matrix([(log2(lanes), *wide(angles(layer, 0), lanes))], 1.0)
        size = count * SUBLANES
        row_pair, block_pair, low_pair = (wide(angles(layer, g), size) for g in (1, 2, 3))
        upper = turn_matrix(
            [(log2(SUBLANES), *row_pair), (log2(n_high), *block_pair), (log2(n_low), *low_pair)], -1.0
        )
        return split(lane), split(upper)

    def mix_in_b(values, lane, upper):
        values = product(upper, split(values.reshape(count * SUBLANES, lanes)))
        return product(split(values), lane).reshape(n_low, n_high, SUBLANES, lanes)

    for load in loads:
        load.wait()

    @pl.loop(0, blocks * rows // 32)
    def _(i):
        t, r = i // (rows // 32), pl.ds(pl.multiple_of(i % (rows // 32) * 32, 32), 32)
        re, im = phase(wave_ref[0, t, r, :], wave_ref[1, t, r, :], level_ref[t, r, :], 0)
        a_ref[0, t, r, :] = re
        a_ref[1, t, r, :] = im

    pl.semaphore_wait(barrier, count - 1)

    def state_copy(j, i):
        k, dh, dl = other(i)
        return pltpu.make_async_remote_copy(
            src_ref=a_ref.at[:, dl, tile(dh, j), :],
            dst_ref=b_ref.at[j, :, ml, mh],
            send_sem=send_sem.at[0],
            recv_sem=recv_state.at[j, k],
            device_id=(dh, dl),
            device_id_type=MESH,
        )

    def level_copy(j, i):
        k, dh, dl = other(i)
        return pltpu.make_async_remote_copy(
            src_ref=level_ref.at[dl, tile(dh, j), :],
            dst_ref=level_b.at[j, ml, mh],
            send_sem=send_sem.at[1],
            recv_sem=recv_level.at[j, k],
            device_id=(dh, dl),
            device_id_type=MESH,
        )

    def back_copy(j, i):
        k, dh, dl = other(i)
        return pltpu.make_async_remote_copy(
            src_ref=c_ref.at[j, :, dl, dh],
            dst_ref=back.at[:, ml, tile(mh, j), :],
            send_sem=send_sem.at[2],
            recv_sem=recv_back.at[j, k],
            device_id=(dh, dl),
            device_id_type=MESH,
        )

    def each(do, copy, j):
        @pl.loop(0, count - 1)
        def _(i):
            getattr(copy(j, i), do)()

    each("start", level_copy, 0)

    @pl.loop(0, chunks)
    def _(j):
        mix_in_a(a_ref, j, 0)

    @pl.loop(0, blocks)
    def _(t):
        for h in range(n_high):
            for p, values in enumerate(mix_chunks(a_ref, t, h, 0)):
                for j, value in enumerate(values):
                    a_ref[p, t, tile(h, j), :] = value

    for j in range(chunks):
        each("start", state_copy, j)
        if j:
            each("start", level_copy, j)
    first, second = tables(0), tables(1)
    for j in range(chunks):
        b_ref[j, :, ml, mh] = a_ref[:, ml, tile(mh, j), :]
        level_b[j, ml, mh] = level_ref[ml, tile(mh, j), :]

    for j in range(chunks):
        each("wait_recv", state_copy, j)
        for p in range(2):
            c_ref[j, p] = mix_in_b(b_ref[j, p], *first)
        each("wait_recv", level_copy, j)

        @pl.loop(0, n_low)
        def _(l):
            re, im = phase(c_ref[j, 0, l], c_ref[j, 1, l], level_b[j, l], 1)
            c_ref[j, 0, l] = re
            c_ref[j, 1, l] = im

        for p in range(2):
            c_ref[j, p] = mix_in_b(c_ref[j, p], *second)
        each("start", back_copy, j)
        back[:, ml, tile(mh, j), :] = c_ref[j, :, ml, mh]

    for j in range(chunks):
        each("wait_recv", back_copy, j)
        mix_in_a(back, j, 1)

    @pl.loop(0, blocks)
    def _(t):
        for h in range(n_high):
            re, im = mix_chunks(back, t, h, 1)
            for j in range(chunks):
                chance[h % 2, h // 2, t, pl.ds(j * SUBLANES, SUBLANES), :] = re[j] * re[j] + im[j] * im[j]

    mz, mc = mh // 2, mh % 2

    def pair_copy(i):
        dz = (mz + i + 1) % twos
        return dz, pltpu.make_async_remote_copy(
            src_ref=chance.at[1 - mc, dz],
            dst_ref=pair.at[dz],
            send_sem=send_sem.at[3],
            recv_sem=recv_pair.at[i],
            device_id=(mz * 2 + 1 - mc, ml),
            device_id_type=MESH,
        )

    def sums_copy(i):
        dz = (mz + i + 1) % twos
        return pltpu.make_async_remote_copy(
            src_ref=sums.at[dz],
            dst_ref=gathered.at[mz],
            send_sem=send_sem.at[4],
            recv_sem=recv_sums.at[i],
            device_id=(dz * 2 + mc, ml),
            device_id_type=MESH,
        )

    for i in range(twos):
        pair_copy(i)[1].start()
    for i in range(twos):
        dz, copy = pair_copy(i)
        copy.wait_recv()
        summed = chance[mc, dz] + pair[dz]
        if i < twos - 1:
            sums[dz] = summed
            sums_copy(i).start()
        else:
            gathered[dz] = summed
    for i in range(twos - 1):
        sums_copy(i).wait_recv()
    for j in range(chunks):
        each("wait_send", state_copy, j)
        each("wait_send", level_copy, j)
        each("wait_send", back_copy, j)
    for i in range(twos):
        pair_copy(i)[1].wait_send()
    for i in range(twos - 1):
        sums_copy(i).wait_send()


def on_device(n_high, n_low, wave_parts, level_table, phase_angles, mix_angles):
    _, blocks, rows, lanes = wave_parts.shape
    if blocks != n_low or n_high % 2 or rows % (n_high * SUBLANES):
        return by_axis(wave_parts, level_table, phase_angles, mix_angles)
    part = rows // n_high
    chunks = part // SUBLANES
    count = n_high * n_low
    f32 = jnp.float32
    vmem = pl.BlockSpec(memory_space=pltpu.VMEM)
    any_space = pl.BlockSpec(memory_space=pl.ANY)
    smem = pl.BlockSpec(memory_space=pltpu.SMEM)
    back, gathered = pl.pallas_call(
        functools.partial(kernel, n_high, n_low),
        out_shape=[
            pltpu.VMEM(wave_parts.shape, f32),
            pltpu.VMEM((n_high // 2, blocks, part, lanes), f32),
        ],
        in_specs=[smem, any_space, any_space, vmem],
        out_specs=[vmem, vmem],
        scratch_shapes=[
            pltpu.VMEM((2, blocks, rows, lanes), f32),
            pltpu.VMEM((blocks, rows, lanes), f32),
            pltpu.VMEM((2, blocks, rows, lanes), f32),
            pltpu.VMEM((chunks, 2, n_low, n_high, SUBLANES, lanes), f32),
            pltpu.VMEM((chunks, 2, n_low, n_high, SUBLANES, lanes), f32),
            pltpu.VMEM((chunks, n_low, n_high, SUBLANES, lanes), f32),
            pltpu.VMEM((2, n_high // 2, blocks, part, lanes), f32),
            pltpu.VMEM((n_high // 2, blocks, part, lanes), f32),
            pltpu.VMEM((n_high // 2, blocks, part, lanes), f32),
            pltpu.SemaphoreType.DMA((2,)),
            pltpu.SemaphoreType.DMA((5,)),
            pltpu.SemaphoreType.DMA((chunks, count)),
            pltpu.SemaphoreType.DMA((chunks, count)),
            pltpu.SemaphoreType.DMA((chunks, count)),
            pltpu.SemaphoreType.DMA((n_high // 2,)),
            pltpu.SemaphoreType.DMA((n_high // 2,)),
        ],
        compiler_params=pltpu.CompilerParams(collective_id=0, has_side_effects=True),
    )(mix_angles, wave_parts, level_table, phase_angles)
    result, marginal = pl.pallas_call(
        functools.partial(finish, n_high),
        out_shape=[
            jax.ShapeDtypeStruct(wave_parts.shape, f32),
            jax.ShapeDtypeStruct((blocks, part, lanes), f32),
        ],
        in_specs=[smem, pl.BlockSpec(memory_space=pltpu.VMEM), pl.BlockSpec(memory_space=pltpu.VMEM)],
        out_specs=[vmem, vmem],
    )(mix_angles, pltpu.with_memory_space_constraint(back, pltpu.VMEM), pltpu.with_memory_space_constraint(gathered, pltpu.VMEM))
    return (result, marginal)


def solution(mesh):
    in_specs = (P(None, ("high", "low"), None, None), P(("high", "low"), None, None), P(), P())
    out_specs = (P(None, ("high", "low"), None, None), P("low", "high", None))
    return jax.shard_map(
        functools.partial(on_device, mesh.shape["high"], mesh.shape["low"]),
        mesh=mesh, in_specs=in_specs, out_specs=out_specs, check_vma=False,
    )
```

profile of v0, /device:TPU:0, one launch (start us, length us, event | category | flops | bytes accessed | tf_op | source)
XLA Modules:
  0.0 50.3 jit_solution(4813169845207830689)
XLA Ops:
  0.6 48.1 %shard_map.59 = (f32[2,4,128,128]{3,2,1,0:T(8,128)S(1)}, f32[4,4,16,128]{3,2,1,0:T(8,128)S(1)}) custom-call(f32[2,4]{1,0:T(2,128)} %mix_ref.3, f32[2,4,128,128]{3,2,1,0:T(8,128)} %wave_hbm.1, f32[4,128,128]{2,1,0:T(8,128)} %level_hbm.1, f32[2,128]{1,0:T(2,128)} %phase_ref.1), custom_call_target="tpu_custom_call" | custom-call | tf_op jit(solution)/shard_map/pallas_call | solution.py:367
  48.7 1.6 %shard_map.60 = (f32[2,4,128,128]{3,2,1,0:T(8,128)}, f32[4,16,128]{2,1,0:T(8,128)}) custom-call(f32[2,4]{1,0:T(2,128)} %mix_ref.3, f32[2,4,128,128]{3,2,1,0:T(8,128)S(1)} %get-tuple-element.4.back, f32[4,4,16,128]{3,2,1,0:T(8,128)S(1)} %get-tuple-element.5.gathered), custom_call_target="tpu_custom_call" | custom-call | tf_op jit(solution)/shard_map/pallas_call | solution.py:395
where the time goes:
time: 50.5 us; the launch traced here: 50.3 us
  Pallas kernels  49.7 us (98%)
  between operations  0.64 us (1%)
    pallas_call x1, Pallas kernels, on_device(): pl.pallas_call(functools.partial(kernel, n_high, n_low), out_shape=[pltpu...  48.1 us
    pallas_call x1, Pallas kernels, on_device(): pl.pallas_call(functools.partial(finish, n_high), out_shape=[jax.ShapeDty...  1.58 us

commit v1 on v0

--- a/solution.py
+++ b/solution.py
@@ -10,6 +10,7 @@
 LAYERS = 2
 MESH = pl.DeviceIdType.MESH
 SUBLANES = 8
+TERMS = 5
 
 
 def count_bits(values, count):
@@ -80,6 +81,23 @@
     return values
 
 
+def series(square, first):
+    terms = [1.0]
+    for n in range(TERMS):
+        terms.append(-terms[-1] / ((2 * n + first) * (2 * n + first + 1)))
+    out = jnp.full_like(square, terms[-1])
+    for term in terms[-2::-1]:
+        out = out * square + term
+    return out
+
+
+def cos_sin(half):
+    square = half * half
+    cos, sin = series(square, 1), half * series(square, 2)
+    twice = sin + sin
+    return 1.0 - twice * sin, twice * cos
+
+
 def turn_matrix(groups, sign):
     size = 1
     for bits, _, _ in groups:
@@ -104,9 +122,8 @@
     return high, (values - high.astype(jnp.float32)).astype(jnp.bfloat16)
 
 
-def product(left, right):
-    dot = functools.partial(jnp.dot, preferred_element_type=jnp.float32)
-    return dot(left[0], right[0]) + (dot(left[1], right[0]) + dot(left[0], right[1]))
+def dot(left, right):
+    return jnp.dot(left, right, preferred_element_type=jnp.float32)
 
 
 def log2(count):
@@ -119,27 +136,22 @@
     return [mix_list([ref[p, t, r, :] for r in at], [(log2(chunks), *pair)]) for p in range(2)]
 
 
-def finish(n_high, mix_ref, back, gathered, out_ref, marginal_ref):
-    _, blocks, rows, lanes = back.shape
-    part = rows // n_high
-    angle = jnp.full((SUBLANES, lanes), mix_ref[LAYERS - 1, 1], jnp.float32)
-    pair = jnp.cos(angle), jnp.sin(angle)
-    for t in range(blocks):
-        for h in range(n_high):
-            for p, values in enumerate(turn_chunks(back, t, h, part, pair)):
-                for j, value in enumerate(values):
-                    out_ref[p, t, pl.ds(h * part + j * SUBLANES, SUBLANES), :] = value
-    total = gathered[0]
-    for z in range(1, gathered.shape[0]):
-        total = total + gathered[z]
-    marginal_ref[...] = total * (1.0 / n_high)
+def finish(back, total, out_hbm, marginal_hbm, sem):
+    copies = [
+        pltpu.make_async_copy(back, out_hbm, sem.at[0]),
+        pltpu.make_async_copy(total, marginal_hbm, sem.at[1]),
+    ]
+    for copy in copies:
+        copy.start()
+    for copy in copies:
+        copy.wait()
 
 
 def kernel(
     n_high, n_low,
     mix_ref, wave_hbm, level_hbm, phase_ref,
-    back, gathered,
-    wave_ref, level_ref, a_ref, b_ref, c_ref, level_b, chance, pair, sums,
+    back, total,
+    wave_ref, level_ref, a_ref, b_ref, c_ref, level_b, chance, pair, sums, gathered,
     load_sem, send_sem, recv_state, recv_level, recv_back, recv_pair, recv_sums,
 ):
     loads = [
@@ -174,8 +186,7 @@
         return tuple(jnp.broadcast_to(x[:1, :1], (size, size)) for x in pair)
 
     def phase(re, im, levels, layer):
-        turn = phase_ref[pl.ds(layer, 1), :] * levels
-        cos, sin = jnp.cos(turn), jnp.sin(turn)
+        cos, sin = cos_sin(phase_ref[pl.ds(layer, 1), :] * 0.5 * levels)
         return re * cos + im * sin, im * cos - re * sin
 
     def tile(h, j):
@@ -194,17 +205,27 @@
         return turn_chunks(ref, t, h, part, angles(layer, 1))
 
     def tables(layer):
-        lane = turn_matrix([(log2(lanes), *wide(angles(layer, 0), lanes))], 1.0)
+        lane = split(turn_matrix([(log2(lanes), *wide(angles(layer, 0), lanes))], 1.0))
+        packed = jnp.concatenate(
+            [jnp.concatenate(lane, axis=1), jnp.concatenate([lane[0], jnp.zeros_like(lane[0])], axis=1)], axis=0
+        )
         size = count * SUBLANES
         row_pair, block_pair, low_pair = (wide(angles(layer, g), size) for g in (1, 2, 3))
         upper = turn_matrix(
             [(log2(SUBLANES), *row_pair), (log2(n_high), *block_pair), (log2(n_low), *low_pair)], -1.0
         )
-        return split(lane), split(upper)
-
-    def mix_in_b(values, lane, upper):
-        values = product(upper, split(values.reshape(count * SUBLANES, lanes)))
-        return product(split(values), lane).reshape(n_low, n_high, SUBLANES, lanes)
+        return packed, split(upper)
+
+    def mix_in_b(ref, j, packed, upper):
+        size = count * SUBLANES
+        both = jnp.concatenate([ref[j, p].reshape(size, lanes) for p in range(2)], axis=1)
+        high, low = split(both)
+        both = dot(upper[0], high) + (dot(upper[1], high) + dot(upper[0], low))
+        rows = jnp.concatenate([both[:, :lanes], both[:, lanes:]], axis=0)
+        out = dot(jnp.concatenate(split(rows), axis=1), packed)
+        out = out[:, :lanes] + out[:, lanes:]
+        for p in range(2):
+            c_ref[j, p] = out[p * size : (p + 1) * size].reshape(n_low, n_high, SUBLANES, lanes)
 
     for load in loads:
         load.wait()
@@ -280,8 +301,7 @@
 
     for j in range(chunks):
         each("wait_recv", state_copy, j)
-        for p in range(2):
-            c_ref[j, p] = mix_in_b(b_ref[j, p], *first)
+        mix_in_b(b_ref, j, *first)
         each("wait_recv", level_copy, j)
 
         @pl.loop(0, n_low)
@@ -290,8 +310,7 @@
             c_ref[j, 0, l] = re
             c_ref[j, 1, l] = im
 
-        for p in range(2):
-            c_ref[j, p] = mix_in_b(c_ref[j, p], *second)
+        mix_in_b(c_ref, j, *second)
         each("start", back_copy, j)
         back[:, ml, tile(mh, j), :] = c_ref[j, :, ml, mh]
 
@@ -304,6 +323,8 @@
         for h in range(n_high):
             re, im = mix_chunks(back, t, h, 1)
             for j in range(chunks):
+                back[0, t, tile(h, j), :] = re[j]
+                back[1, t, tile(h, j), :] = im[j]
                 chance[h % 2, h // 2, t, pl.ds(j * SUBLANES, SUBLANES), :] = re[j] * re[j] + im[j] * im[j]
 
     mz, mc = mh // 2, mh % 2
@@ -343,6 +364,10 @@
             gathered[dz] = summed
     for i in range(twos - 1):
         sums_copy(i).wait_recv()
+    summed = gathered[0]
+    for z in range(1, twos):
+        summed = summed + gathered[z]
+    total[...] = summed * (1.0 / n_high)
     for j in range(chunks):
         each("wait_send", state_copy, j)
         each("wait_send", level_copy, j)
@@ -364,11 +389,11 @@
     vmem = pl.BlockSpec(memory_space=pltpu.VMEM)
     any_space = pl.BlockSpec(memory_space=pl.ANY)
     smem = pl.BlockSpec(memory_space=pltpu.SMEM)
-    back, gathered = pl.pallas_call(
+    back, total = pl.pallas_call(
         functools.partial(kernel, n_high, n_low),
         out_shape=[
             pltpu.VMEM(wave_parts.shape, f32),
-            pltpu.VMEM((n_high // 2, blocks, part, lanes), f32),
+            pltpu.VMEM((blocks, part, lanes), f32),
         ],
         in_specs=[smem, any_space, any_space, vmem],
         out_specs=[vmem, vmem],
@@ -382,6 +407,7 @@
             pltpu.VMEM((2, n_high // 2, blocks, part, lanes), f32),
             pltpu.VMEM((n_high // 2, blocks, part, lanes), f32),
             pltpu.VMEM((n_high // 2, blocks, part, lanes), f32),
+            pltpu.VMEM((n_high // 2, blocks, part, lanes), f32),
             pltpu.SemaphoreType.DMA((2,)),
             pltpu.SemaphoreType.DMA((5,)),
             pltpu.SemaphoreType.DMA((chunks, count)),
@@ -393,14 +419,15 @@
         compiler_params=pltpu.CompilerParams(collective_id=0, has_side_effects=True),
     )(mix_angles, wave_parts, level_table, phase_angles)
     result, marginal = pl.pallas_call(
-        functools.partial(finish, n_high),
+        finish,
         out_shape=[
             jax.ShapeDtypeStruct(wave_parts.shape, f32),
             jax.ShapeDtypeStruct((blocks, part, lanes), f32),
         ],
-        in_specs=[smem, pl.BlockSpec(memory_space=pltpu.VMEM), pl.BlockSpec(memory_space=pltpu.VMEM)],
-        out_specs=[vmem, vmem],
-    )(mix_angles, pltpu.with_memory_space_constraint(back, pltpu.VMEM), pltpu.with_memory_space_constraint(gathered, pltpu.VMEM))
+        in_specs=[vmem, vmem],
+        out_specs=[any_space, any_space],
+        scratch_shapes=[pltpu.SemaphoreType.DMA((2,))],
+    )(*(pltpu.with_memory_space_constraint(x, pltpu.VMEM) for x in (back, total)))
     return (result, marginal)
 
 

time: 50.5 us -> 49.3 us (0.976)
  Pallas kernels: 49.7 us -> 48.5 us
    pallas_call x1, Pallas kernels: 1.58 us -> 0.81 us  [on_device(): pl.pallas_call(finish, out_shape=[jax.ShapeDtypeStruct(wave_parts.shape,...]
where the time goes in v1:
time: 49.3 us; the launch traced here: 49.1 us
  Pallas kernels  48.5 us (98%)
  between operations  0.64 us (1%)
    pallas_call x1, Pallas kernels, on_device(): pl.pallas_call(functools.partial(kernel, n_high, n_low), out_shape=[pltpu...  47.6 us

profile of v1, /device:TPU:0, one launch (start us, length us, event | category | flops | bytes accessed | tf_op | source)
XLA Modules:
  0.0 49.1 jit_solution(7436170710578270156)
XLA Ops:
  0.6 47.6 %shard_map.59 = (f32[2,4,128,128]{3,2,1,0:T(8,128)S(1)}, f32[4,16,128]{2,1,0:T(8,128)S(1)}) custom-call(f32[2,4]{1,0:T(2,128)} %mix_ref.1, f32[2,4,128,128]{3,2,1,0:T(8,128)} %wave_hbm.1, f32[4,128,128]{2,1,0:T(8,128)} %level_hbm.1, f32[2,128]{1,0:T(2,128)} %phase_ref.1), custom_call_target="tpu_custom_call" | custom-call | tf_op jit(solution)/shard_map/pallas_call | solution.py:392
  48.3 0.8 %shard_map.60 = (f32[2,4,128,128]{3,2,1,0:T(8,128)}, f32[4,16,128]{2,1,0:T(8,128)}) custom-call(f32[2,4,128,128]{3,2,1,0:T(8,128)S(1)} %get-tuple-element.4.back, f32[4,16,128]{2,1,0:T(8,128)S(1)} %get-tuple-element.5.total), custom_call_target="tpu_custom_call" | custom-call | tf_op jit(solution)/shard_map/pallas_call | solution.py:421

commit v2 on v1

--- a/solution.py
+++ b/solution.py
@@ -126,6 +126,10 @@
     return jnp.dot(left, right, preferred_element_type=jnp.float32)
 
 
+def doublings(first, end):
+    return [1 << i for i in range(first.bit_length() - 1, end.bit_length() - 1)]
+
+
 def log2(count):
     return count.bit_length() - 1
 
@@ -151,8 +155,8 @@
     n_high, n_low,
     mix_ref, wave_hbm, level_hbm, phase_ref,
     back, total,
-    wave_ref, level_ref, a_ref, b_ref, c_ref, level_b, chance, pair, sums, gathered,
-    load_sem, send_sem, recv_state, recv_level, recv_back, recv_pair, recv_sums,
+    wave_ref, level_ref, level_far, a_ref, b_ref, c_ref, level_b, chance, pair, sums, gathered,
+    ready, load_sem, send_sem, recv_far, recv_state, recv_level, recv_back, recv_pair, recv_sums,
 ):
     loads = [
         pltpu.make_async_copy(level_hbm, level_ref, load_sem.at[0]),
@@ -164,7 +168,7 @@
     part = rows // n_high
     chunks = part // SUBLANES
     count = n_high * n_low
-    twos = n_high // 2
+    twos = half = n_high // 2
     mh, ml = lax.axis_index("high"), lax.axis_index("low")
 
     barrier = pltpu.get_barrier_semaphore()
@@ -173,10 +177,20 @@
         k = 1 + i
         return k, (mh + k // n_low) % n_high, (ml + k % n_low) % n_low
 
-    @pl.loop(0, count - 1)
+    def flip(value, bit):
+        return value + bit * (1 - 2 * (value // bit % 2))
+
+    mz, mc = mh // 2, mh % 2
+    far = (mh + half) % n_high
+    mine = mh // half * half
+
+    @pl.loop(1, 2 * n_low)
     def _(i):
-        _, dh, dl = other(i)
+        dh, dl = mz * 2 + (mc + i // n_low) % 2, (ml + i % n_low) % n_low
         pl.semaphore_signal(barrier, inc=1, device_id=(dh, dl), device_id_type=MESH)
+
+    for bit in doublings(2, n_high):
+        pl.semaphore_signal(barrier, inc=1, device_id=(flip(mh, bit), ml), device_id_type=MESH)
 
     def angles(layer, group):
         angle = jnp.full((SUBLANES, lanes), mix_ref[layer, group], jnp.float32)
@@ -191,6 +205,9 @@
 
     def tile(h, j):
         return pl.ds(pl.multiple_of(h * part + j * SUBLANES, SUBLANES), SUBLANES)
+
+    def rows_of(h):
+        return pl.ds(pl.multiple_of(h * part, SUBLANES), part)
 
     def mix_in_a(ref, j, layer):
         row_pair, block_pair = angles(layer, 1), angles(layer, 2)
@@ -227,18 +244,6 @@
         for p in range(2):
             c_ref[j, p] = out[p * size : (p + 1) * size].reshape(n_low, n_high, SUBLANES, lanes)
 
-    for load in loads:
-        load.wait()
-
-    @pl.loop(0, blocks * rows // 32)
-    def _(i):
-        t, r = i // (rows // 32), pl.ds(pl.multiple_of(i % (rows // 32) * 32, 32), 32)
-        re, im = phase(wave_ref[0, t, r, :], wave_ref[1, t, r, :], level_ref[t, r, :], 0)
-        a_ref[0, t, r, :] = re
-        a_ref[1, t, r, :] = im
-
-    pl.semaphore_wait(barrier, count - 1)
-
     def state_copy(j, i):
         k, dh, dl = other(i)
         return pltpu.make_async_remote_copy(
@@ -250,14 +255,25 @@
             device_id_type=MESH,
         )
 
-    def level_copy(j, i):
-        k, dh, dl = other(i)
+    def far_copy(t):
         return pltpu.make_async_remote_copy(
-            src_ref=level_ref.at[dl, tile(dh, j), :],
-            dst_ref=level_b.at[j, ml, mh],
+            src_ref=level_ref.at[t, pl.ds(pl.multiple_of((half - mine) * part, SUBLANES), half * part), :],
+            dst_ref=level_far.at[t],
+            send_sem=send_sem.at[5],
+            recv_sem=recv_far.at[t],
+            device_id=(far, ml),
+            device_id_type=MESH,
+        )
+
+    def level_copy(whose, i):
+        k = 1 + i
+        dh, dl = (mh - mine + k // n_low) % half, (ml + k % n_low) % n_low
+        return pltpu.make_async_remote_copy(
+            src_ref=[level_ref.at[dl, rows_of(mine + dh), :], level_far.at[dl, rows_of(dh), :]][whose],
+            dst_ref=level_b.at[ml, [mh, far][whose]],
             send_sem=send_sem.at[1],
-            recv_sem=recv_level.at[j, k],
-            device_id=(dh, dl),
+            recv_sem=recv_level.at[whose, k],
+            device_id=(mine + dh, dl),
             device_id_type=MESH,
         )
 
@@ -273,11 +289,35 @@
         )
 
     def each(do, copy, j):
-        @pl.loop(0, count - 1)
+        @pl.loop(0, half * n_low - 1 if copy is level_copy else count - 1)
         def _(i):
             getattr(copy(j, i), do)()
 
-    each("start", level_copy, 0)
+    bits = doublings(2, n_high)
+
+    def tell(i):
+        pl.semaphore_signal(ready.at[i], inc=1, device_id=(flip(mh, bits[i]), ml), device_id_type=MESH)
+
+    def hear(i):
+        pl.semaphore_wait(ready.at[i], 1)
+
+    loads[0].wait()
+    pl.semaphore_wait(barrier, 2 * n_low - 1 + len(bits))
+    for t in range(blocks):
+        far_copy(t).start()
+    tell(0)
+    loads[1].wait()
+
+    @pl.loop(0, blocks * rows // 32)
+    def _(i):
+        t, r = i // (rows // 32), pl.ds(pl.multiple_of(i % (rows // 32) * 32, 32), 32)
+        re, im = phase(wave_ref[0, t, r, :], wave_ref[1, t, r, :], level_ref[t, r, :], 0)
+        a_ref[0, t, r, :] = re
+        a_ref[1, t, r, :] = im
+
+    for i in range(1, len(bits)):
+        hear(i - 1)
+        tell(i)
 
     @pl.loop(0, chunks)
     def _(j):
@@ -290,23 +330,31 @@
                 for j, value in enumerate(values):
                     a_ref[p, t, tile(h, j), :] = value
 
-    for j in range(chunks):
-        each("start", state_copy, j)
-        if j:
-            each("start", level_copy, j)
+    hear(len(bits) - 1)
+    each("start", state_copy, 0)
+    each("start", level_copy, 0)
     first, second = tables(0), tables(1)
     for j in range(chunks):
         b_ref[j, :, ml, mh] = a_ref[:, ml, tile(mh, j), :]
-        level_b[j, ml, mh] = level_ref[ml, tile(mh, j), :]
+    level_b[ml, mh] = level_ref[ml, rows_of(mh), :]
+    for t in range(blocks):
+        far_copy(t).wait_recv()
+    each("start", level_copy, 1)
+    for j in range(1, chunks):
+        each("start", state_copy, j)
+    level_b[ml, far] = level_far[ml, rows_of(mh - mine), :]
 
     for j in range(chunks):
         each("wait_recv", state_copy, j)
         mix_in_b(b_ref, j, *first)
-        each("wait_recv", level_copy, j)
+        if j == 0:
+            each("wait_recv", level_copy, 0)
+            each("wait_recv", level_copy, 1)
 
         @pl.loop(0, n_low)
         def _(l):
-            re, im = phase(c_ref[j, 0, l], c_ref[j, 1, l], level_b[j, l], 1)
+            levels = level_b[l, :, j * SUBLANES : (j + 1) * SUBLANES, :]
+            re, im = phase(c_ref[j, 0, l], c_ref[j, 1, l], levels, 1)
             c_ref[j, 0, l] = re
             c_ref[j, 1, l] = im
 
@@ -326,8 +374,6 @@
                 back[0, t, tile(h, j), :] = re[j]
                 back[1, t, tile(h, j), :] = im[j]
                 chance[h % 2, h // 2, t, pl.ds(j * SUBLANES, SUBLANES), :] = re[j] * re[j] + im[j] * im[j]
-
-    mz, mc = mh // 2, mh % 2
 
     def pair_copy(i):
         dz = (mz + i + 1) % twos
@@ -370,8 +416,11 @@
     total[...] = summed * (1.0 / n_high)
     for j in range(chunks):
         each("wait_send", state_copy, j)
-        each("wait_send", level_copy, j)
         each("wait_send", back_copy, j)
+    for whose in range(2):
+        each("wait_send", level_copy, whose)
+    for t in range(blocks):
+        far_copy(t).wait_send()
     for i in range(twos):
         pair_copy(i)[1].wait_send()
     for i in range(twos - 1):
@@ -380,7 +429,7 @@
 
 def on_device(n_high, n_low, wave_parts, level_table, phase_angles, mix_angles):
     _, blocks, rows, lanes = wave_parts.shape
-    if blocks != n_low or n_high % 2 or rows % (n_high * SUBLANES):
+    if blocks != n_low or n_high < 4 or n_high & (n_high - 1) or rows % (n_high * SUBLANES):
         return by_axis(wave_parts, level_table, phase_angles, mix_angles)
     part = rows // n_high
     chunks = part // SUBLANES
@@ -400,18 +449,21 @@
         scratch_shapes=[
             pltpu.VMEM((2, blocks, rows, lanes), f32),
             pltpu.VMEM((blocks, rows, lanes), f32),
+            pltpu.VMEM((blocks, rows // 2, lanes), f32),
             pltpu.VMEM((2, blocks, rows, lanes), f32),
             pltpu.VMEM((chunks, 2, n_low, n_high, SUBLANES, lanes), f32),
             pltpu.VMEM((chunks, 2, n_low, n_high, SUBLANES, lanes), f32),
-            pltpu.VMEM((chunks, n_low, n_high, SUBLANES, lanes), f32),
+            pltpu.VMEM((n_low, n_high, part, lanes), f32),
             pltpu.VMEM((2, n_high // 2, blocks, part, lanes), f32),
             pltpu.VMEM((n_high // 2, blocks, part, lanes), f32),
             pltpu.VMEM((n_high // 2, blocks, part, lanes), f32),
             pltpu.VMEM((n_high // 2, blocks, part, lanes), f32),
+            pltpu.SemaphoreType.REGULAR((log2(n_high) - 1,)),
             pltpu.SemaphoreType.DMA((2,)),
-            pltpu.SemaphoreType.DMA((5,)),
+            pltpu.SemaphoreType.DMA((6,)),
+            pltpu.SemaphoreType.DMA((blocks,)),
             pltpu.SemaphoreType.DMA((chunks, count)),
-            pltpu.SemaphoreType.DMA((chunks, count)),
+            pltpu.SemaphoreType.DMA((2, count // 2)),
             pltpu.SemaphoreType.DMA((chunks, count)),
             pltpu.SemaphoreType.DMA((n_high // 2,)),
             pltpu.SemaphoreType.DMA((n_high // 2,)),

time: 49.3 us -> 46.8 us (0.949)
  Pallas kernels: 48.5 us -> 46 us
    pallas_call x1, Pallas kernels: 47.6 us -> 45.2 us  [on_device(): pl.pallas_call(functools.partial(kernel, n_high, n_low), out_shape=[pltpu...]
where the time goes in v2:
time: 46.8 us; the launch traced here: 46.6 us
  Pallas kernels  46 us (98%)
  between operations  0.64 us (1%)
    pallas_call x1, Pallas kernels, on_device(): pl.pallas_call(functools.partial(kernel, n_high, n_low), out_shape=[pltpu...  45.2 us

profile of v2, /device:TPU:0, one launch (start us, length us, event | category | flops | bytes accessed | tf_op | source)
XLA Modules:
  0.0 46.6 jit_solution(14244358510959263415)
XLA Ops:
  0.6 45.2 %shard_map.59 = (f32[2,4,128,128]{3,2,1,0:T(8,128)S(1)}, f32[4,16,128]{2,1,0:T(8,128)S(1)}) custom-call(f32[2,4]{1,0:T(2,128)} %mix_ref.1, f32[2,4,128,128]{3,2,1,0:T(8,128)} %wave_hbm.1, f32[4,128,128]{2,1,0:T(8,128)} %level_hbm.1, f32[2,128]{1,0:T(2,128)} %phase_ref.1), custom_call_target="tpu_custom_call" | custom-call | tf_op jit(solution)/shard_map/pallas_call | solution.py:441
  45.8 0.8 %shard_map.60 = (f32[2,4,128,128]{3,2,1,0:T(8,128)}, f32[4,16,128]{2,1,0:T(8,128)}) custom-call(f32[2,4,128,128]{3,2,1,0:T(8,128)S(1)} %get-tuple-element.4.back, f32[4,16,128]{2,1,0:T(8,128)S(1)} %get-tuple-element.5.total), custom_call_target="tpu_custom_call" | custom-call | tf_op jit(solution)/shard_map/pallas_call | solution.py:473

commit v3 on v2

--- a/solution.py
+++ b/solution.py
@@ -126,6 +126,12 @@
     return jnp.dot(left, right, preferred_element_type=jnp.float32)
 
 
+def spread(count):
+    even, odd = list(range(2, count, 2)), list(range(1, count, 2))
+    middle = len(even) // 2
+    return even[:middle] + even[middle + 1 :] + even[middle : middle + 1] + odd + [0]
+
+
 def doublings(first, end):
     return [1 << i for i in range(first.bit_length() - 1, end.bit_length() - 1)]
 
@@ -289,8 +295,8 @@
         )
 
     def each(do, copy, j):
-        @pl.loop(0, half * n_low - 1 if copy is level_copy else count - 1)
-        def _(i):
+        planes = range(half) if copy is level_copy else spread(n_high)
+        for i in [h * n_low + l - 1 for h in planes for l in range(n_low) if h or l]:
             getattr(copy(j, i), do)()
 
     bits = doublings(2, n_high)
@@ -363,6 +369,13 @@
         back[:, ml, tile(mh, j), :] = c_ref[j, :, ml, mh]
 
     for j in range(chunks):
+        each("wait_send", state_copy, j)
+    for whose in range(2):
+        each("wait_send", level_copy, whose)
+    for t in range(blocks):
+        far_copy(t).wait_send()
+
+    for j in range(chunks):
         each("wait_recv", back_copy, j)
         mix_in_a(back, j, 1)
 
@@ -378,7 +391,7 @@
     def pair_copy(i):
         dz = (mz + i + 1) % twos
         return dz, pltpu.make_async_remote_copy(
-            src_ref=chance.at[1 - mc, dz],
+            src_ref=chance.at[mc, dz],
             dst_ref=pair.at[dz],
             send_sem=send_sem.at[3],
             recv_sem=recv_pair.at[i],
@@ -393,7 +406,7 @@
             dst_ref=gathered.at[mz],
             send_sem=send_sem.at[4],
             recv_sem=recv_sums.at[i],
-            device_id=(dz * 2 + mc, ml),
+            device_id=(dz * 2 + 1 - mc, ml),
             device_id_type=MESH,
         )
 
@@ -402,28 +415,19 @@
     for i in range(twos):
         dz, copy = pair_copy(i)
         copy.wait_recv()
-        summed = chance[mc, dz] + pair[dz]
-        if i < twos - 1:
-            sums[dz] = summed
-            sums_copy(i).start()
-        else:
-            gathered[dz] = summed
-    for i in range(twos - 1):
+        sums[dz] = chance[1 - mc, dz] + pair[dz]
+        sums_copy(i).start()
+    for j in range(chunks):
+        each("wait_send", back_copy, j)
+    for i in range(twos):
+        pair_copy(i)[1].wait_send()
+    for i in range(twos):
         sums_copy(i).wait_recv()
     summed = gathered[0]
     for z in range(1, twos):
         summed = summed + gathered[z]
     total[...] = summed * (1.0 / n_high)
-    for j in range(chunks):
-        each("wait_send", state_copy, j)
-        each("wait_send", back_copy, j)
-    for whose in range(2):
-        each("wait_send", level_copy, whose)
-    for t in range(blocks):
-        far_copy(t).wait_send()
     for i in range(twos):
-        pair_copy(i)[1].wait_send()
-    for i in range(twos - 1):
         sums_copy(i).wait_send()
 
 

time: 46.8 us -> 45.5 us (0.972)
  Pallas kernels: 46 us -> 44.7 us
    pallas_call x1, Pallas kernels: 45.2 us -> 43.9 us  [on_device(): pl.pallas_call(functools.partial(kernel, n_high, n_low), out_shape=[pltpu...]
where the time goes in v3:
time: 45.5 us; the launch traced here: 45.3 us
  Pallas kernels  44.7 us (98%)
  between operations  0.64 us (1%)
    pallas_call x1, Pallas kernels, on_device(): pl.pallas_call(functools.partial(kernel, n_high, n_low), out_shape=[pltpu...  43.9 us

profile of v3, /device:TPU:0, one launch (start us, length us, event | category | flops | bytes accessed | tf_op | source)
XLA Modules:
  0.0 45.3 jit_solution(6655656539442689071)
XLA Ops:
  0.6 43.9 %shard_map.59 = (f32[2,4,128,128]{3,2,1,0:T(8,128)S(1)}, f32[4,16,128]{2,1,0:T(8,128)S(1)}) custom-call(f32[2,4]{1,0:T(2,128)} %mix_ref.1, f32[2,4,128,128]{3,2,1,0:T(8,128)} %wave_hbm.1, f32[4,128,128]{2,1,0:T(8,128)} %level_hbm.1, f32[2,128]{1,0:T(2,128)} %phase_ref.1), custom_call_target="tpu_custom_call" | custom-call | tf_op jit(solution)/shard_map/pallas_call | solution.py:445
  44.5 0.8 %shard_map.60 = (f32[2,4,128,128]{3,2,1,0:T(8,128)}, f32[4,16,128]{2,1,0:T(8,128)}) custom-call(f32[2,4,128,128]{3,2,1,0:T(8,128)S(1)} %get-tuple-element.4.back, f32[4,16,128]{2,1,0:T(8,128)S(1)} %get-tuple-element.5.total), custom_call_target="tpu_custom_call" | custom-call | tf_op jit(solution)/shard_map/pallas_call | solution.py:477

commit v4 on v3

--- a/solution.py
+++ b/solution.py
@@ -126,10 +126,11 @@
     return jnp.dot(left, right, preferred_element_type=jnp.float32)
 
 
-def spread(count):
-    even, odd = list(range(2, count, 2)), list(range(1, count, 2))
-    middle = len(even) // 2
-    return even[:middle] + even[middle + 1 :] + even[middle : middle + 1] + odd + [0]
+def xor(left, right):
+    out = 0
+    for bit in doublings(1, 64):
+        out = out + (left // bit + right // bit) % 2 * bit
+    return out
 
 
 def doublings(first, end):
@@ -159,14 +160,16 @@
 
 def kernel(
     n_high, n_low,
-    mix_ref, wave_hbm, level_hbm, phase_ref,
+    mix_hbm, wave_hbm, level_hbm, phase_hbm,
     back, total,
-    wave_ref, level_ref, level_far, a_ref, b_ref, c_ref, level_b, chance, pair, sums, gathered,
+    mix_ref, phase_ref, wave_ref, level_ref, level_far, a_ref, b_ref, c_ref, level_b, chance, pair, sums, gathered,
     ready, load_sem, send_sem, recv_far, recv_state, recv_level, recv_back, recv_pair, recv_sums,
 ):
     loads = [
         pltpu.make_async_copy(level_hbm, level_ref, load_sem.at[0]),
         pltpu.make_async_copy(wave_hbm, wave_ref, load_sem.at[1]),
+        pltpu.make_async_copy(phase_hbm, phase_ref, load_sem.at[2]),
+        pltpu.make_async_copy(mix_hbm, mix_ref, load_sem.at[3]),
     ]
     for load in loads:
         load.start()
@@ -183,20 +186,17 @@
         k = 1 + i
         return k, (mh + k // n_low) % n_high, (ml + k % n_low) % n_low
 
-    def flip(value, bit):
-        return value + bit * (1 - 2 * (value // bit % 2))
-
     mz, mc = mh // 2, mh % 2
     far = (mh + half) % n_high
     mine = mh // half * half
 
-    @pl.loop(1, 2 * n_low)
-    def _(i):
-        dh, dl = mz * 2 + (mc + i // n_low) % 2, (ml + i % n_low) % n_low
-        pl.semaphore_signal(barrier, inc=1, device_id=(dh, dl), device_id_type=MESH)
-
-    for bit in doublings(2, n_high):
-        pl.semaphore_signal(barrier, inc=1, device_id=(flip(mh, bit), ml), device_id_type=MESH)
+    steps = [(bit, 0) for bit in doublings(1, n_high)] + [(0, bit) for bit in doublings(1, n_low)]
+
+    def across(step):
+        return xor(mh, step[0]), xor(ml, step[1])
+
+    for step in steps:
+        pl.semaphore_signal(barrier, inc=1, device_id=across(step), device_id_type=MESH)
 
     def angles(layer, group):
         angle = jnp.full((SUBLANES, lanes), mix_ref[layer, group], jnp.float32)
@@ -295,24 +295,27 @@
         )
 
     def each(do, copy, j):
-        planes = range(half) if copy is level_copy else spread(n_high)
-        for i in [h * n_low + l - 1 for h in planes for l in range(n_low) if h or l]:
+        for i in range(half * n_low - 1 if copy is level_copy else count - 1):
             getattr(copy(j, i), do)()
 
-    bits = doublings(2, n_high)
+    rounds = [step for step in steps if step != (half, 0)]
 
     def tell(i):
-        pl.semaphore_signal(ready.at[i], inc=1, device_id=(flip(mh, bits[i]), ml), device_id_type=MESH)
+        pl.semaphore_signal(ready.at[i], inc=1, device_id=across(rounds[i]), device_id_type=MESH)
 
     def hear(i):
         pl.semaphore_wait(ready.at[i], 1)
 
     loads[0].wait()
-    pl.semaphore_wait(barrier, 2 * n_low - 1 + len(bits))
+    pl.semaphore_wait(barrier, len(steps))
     for t in range(blocks):
         far_copy(t).start()
     tell(0)
-    loads[1].wait()
+    for load in loads[1:]:
+        load.wait()
+    for i in range(1, len(rounds) - 1):
+        hear(i - 1)
+        tell(i)
 
     @pl.loop(0, blocks * rows // 32)
     def _(i):
@@ -321,9 +324,8 @@
         a_ref[0, t, r, :] = re
         a_ref[1, t, r, :] = im
 
-    for i in range(1, len(bits)):
-        hear(i - 1)
-        tell(i)
+    hear(len(rounds) - 2)
+    tell(len(rounds) - 1)
 
     @pl.loop(0, chunks)
     def _(j):
@@ -336,7 +338,7 @@
                 for j, value in enumerate(values):
                     a_ref[p, t, tile(h, j), :] = value
 
-    hear(len(bits) - 1)
+    hear(len(rounds) - 1)
     each("start", state_copy, 0)
     each("start", level_copy, 0)
     first, second = tables(0), tables(1)
@@ -441,16 +443,17 @@
     f32 = jnp.float32
     vmem = pl.BlockSpec(memory_space=pltpu.VMEM)
     any_space = pl.BlockSpec(memory_space=pl.ANY)
-    smem = pl.BlockSpec(memory_space=pltpu.SMEM)
     back, total = pl.pallas_call(
         functools.partial(kernel, n_high, n_low),
         out_shape=[
             pltpu.VMEM(wave_parts.shape, f32),
             pltpu.VMEM((blocks, part, lanes), f32),
         ],
-        in_specs=[smem, any_space, any_space, vmem],
+        in_specs=[any_space] * 4,
         out_specs=[vmem, vmem],
         scratch_shapes=[
+            pltpu.SMEM(mix_angles.shape, f32),
+            pltpu.VMEM(phase_angles.shape, f32),
             pltpu.VMEM((2, blocks, rows, lanes), f32),
             pltpu.VMEM((blocks, rows, lanes), f32),
             pltpu.VMEM((blocks, rows // 2, lanes), f32),
@@ -462,8 +465,8 @@
             pltpu.VMEM((n_high // 2, blocks, part, lanes), f32),
             pltpu.VMEM((n_high // 2, blocks, part, lanes), f32),
             pltpu.VMEM((n_high // 2, blocks, part, lanes), f32),
-            pltpu.SemaphoreType.REGULAR((log2(n_high) - 1,)),
-            pltpu.SemaphoreType.DMA((2,)),
+            pltpu.SemaphoreType.REGULAR((log2(count) - 1,)),
+            pltpu.SemaphoreType.DMA((4,)),
             pltpu.SemaphoreType.DMA((6,)),
             pltpu.SemaphoreType.DMA((blocks,)),
             pltpu.SemaphoreType.DMA((chunks, count)),

time: 45.5 us -> 44.2 us (0.971)
  Pallas kernels: 44.7 us -> 43.2 us
    pallas_call x1, Pallas kernels: 43.9 us -> 42.3 us  [on_device(): pl.pallas_call(functools.partial(kernel, n_high, n_low), out_shape=[pltpu...]
where the time goes in v4:
time: 44.2 us; the launch traced here: 43.8 us
  Pallas kernels  43.2 us (98%)
  between operations  0.64 us (1%)
    pallas_call x1, Pallas kernels, on_device(): pl.pallas_call(functools.partial(kernel, n_high, n_low), out_shape=[pltpu...  42.3 us

profile of v4, /device:TPU:0, one launch (start us, length us, event | category | flops | bytes accessed | tf_op | source)
XLA Modules:
  0.0 43.8 jit_solution(7952728008986441465)
XLA Ops:
  0.6 42.3 %shard_map.59 = (f32[2,4,128,128]{3,2,1,0:T(8,128)S(1)}, f32[4,16,128]{2,1,0:T(8,128)S(1)}) custom-call(f32[2,4]{1,0:T(2,128)} %mix_hbm.1, f32[2,4,128,128]{3,2,1,0:T(8,128)} %wave_hbm.1, f32[4,128,128]{2,1,0:T(8,128)} %level_hbm.1, f32[2,128]{1,0:T(2,128)} %phase_hbm.1), custom_call_target="tpu_custom_call" | custom-call | tf_op jit(solution)/shard_map/pallas_call | solution.py:446
  43.0 0.8 %shard_map.60 = (f32[2,4,128,128]{3,2,1,0:T(8,128)}, f32[4,16,128]{2,1,0:T(8,128)}) custom-call(f32[2,4,128,128]{3,2,1,0:T(8,128)S(1)} %get-tuple-element.4.back, f32[4,16,128]{2,1,0:T(8,128)S(1)} %get-tuple-element.5.total), custom_call_target="tpu_custom_call" | custom-call | tf_op jit(solution)/shard_map/pallas_call | solution.py:480
